TPU v7x, 128 devices: a whole 4x4x4 slice. The times are simulated.
128 devices in a mesh: row: 8 (over z_lo, y), col: 16 (over z_hi, x, core).
Axes of the slice: x: 4, y: 4, z: 4 (z_hi: 2, z_lo: 2; z = z_hi * 2 + z_lo), core: 2. Of those that a mesh axis runs over, the one named last changes fastest.
Arguments:
- vorticity: float32 [3, 128, 128, 128], P(None, 'row', 'col'), may hold values from -18.1 to 18.1
- scalar: float32 [256, 256, 256], P('row', 'col'), may hold values from -6 to 6
Outputs:
- advected: float32 [256, 256, 256], P('row', 'col')
All inputs are finite; a program needn't handle non-finite values. Where the computation divides by a largest or mean magnitude, that divisor is 1e-20 or more.
Results may differ from a plain program's by a relative error of at most 0.0003.
Values sent between devices are 32-bit elements; how exact they have to be, the bound alone decides.
A program may use at most 64 MiB of HBM per device.

v0:
```python
import functools
import math

import jax
import jax.numpy as jnp
import numpy as np
from jax import lax
from jax.experimental import pallas as pl
from jax.experimental.pallas import tpu as pltpu
from jax.sharding import PartitionSpec as P

COURANT = 0.9
EPSILON = 1e-06
MESH = pl.DeviceIdType.MESH
HIGH = lax.Precision.HIGH

N = 128
ROWS, COLS = 8, 16
CHIPS = 64
YB, ZB = 16, 8
FY, FZ = 32, 16
EY, EZ = 38, 24


def turn(exponent):
    angle = 2.0 * math.pi * np.asarray(exponent, np.float64)
    return np.cos(angle), np.sin(angle)


def left_block(re, im):
    return np.block([[re, -im], [im, re]]).astype(np.float32)


def right_block(re, im):
    return np.block([[re, im], [-im, re]]).astype(np.float32)


@functools.cache
def spectral_tables():
    x = np.arange(N)
    k = np.arange(N // 2)
    cos, sin = turn(k[:, None] * x[None, :] / N)
    forward_x = np.concatenate([cos, -sin]).astype(np.float32)
    weight = np.where(k == 0, 1.0, 2.0)[:, None]
    inverse_x = np.concatenate([weight * cos, -weight * sin]).astype(np.float32)
    high = np.arange(64) // 8
    low = np.arange(64) % 8
    grid = (high[:, None] * high[None, :] + low[:, None] * low[None, :]) / 8.0
    forward_left, inverse_left = [], []
    for core in range(2):
        shift = low * (1 - core) / 16.0
        forward_left.append(left_block(*turn(-(grid + shift[:, None]))))
        inverse_left.append(left_block(*turn(grid + shift[None, :])))
    lane = np.arange(N)
    lane_y, lane_z = lane // 8, lane % 8
    lanes = lane_y[:, None] * lane_y[None, :] / 16.0 + lane_z[:, None] * lane_z[None, :] / 8.0
    forward_right = right_block(*turn(-lanes))
    inverse_right = right_block(*turn(lanes))
    twiddle = []
    waves = []
    for core in range(2):
        phase = high[:, None] * lane_y[None, :] + (low + 8 * core)[:, None] * lane_z[None, :]
        twiddle.append(np.stack(turn(-phase / N)))
        ky = high[:, None] + 8 * lane_y[None, :]
        kz = (low + 8 * core)[:, None] + 16 * lane_z[None, :]
        waves.append(np.stack([np.where(q < N // 2, q, q - N) for q in (ky, kz)]))
    return (
        forward_x,
        np.stack(forward_left),
        np.stack(twiddle).astype(np.float32),
        forward_right,
        np.stack(waves).astype(np.float32),
        inverse_right,
        np.stack(inverse_left),
        inverse_x,
    )


@functools.cache
def refine_tables():
    lines = np.zeros((N, 2 * N))
    for fine in range(2 * N):
        coarse = fine // 2
        lines[coarse, fine] += 0.75
        lines[(coarse + (1 if fine % 2 else -1)) % N, fine] += 0.25
    place = {}
    for y in range(YB):
        for z in range(ZB):
            place[y, z] = y * ZB + z
    for i in range(2):
        for z in range(ZB):
            place[i - 2, z] = 128 + i * ZB + z
            place[YB + i, z] = 144 + i * ZB + z
        for y in range(YB):
            place[y, i - 2] = 160 + i * YB + y
            place[y, ZB + i] = 192 + i * YB + y
    for index, (ys, zs) in enumerate(((-2, -2), (-2, ZB), (YB, -2), (YB, ZB))):
        for i in range(2):
            for j in range(2):
                place[ys + j, zs + i] = 224 + 8 * index + 2 * i + j

    def taps(fine):
        coarse = fine // 2
        return ((coarse, 0.75), (coarse + (1 if fine % 2 else -1), 0.25))

    slots = list(range(FZ)) + [16, 17, 18, None, None, -3, -2, -1]
    block = np.zeros((EY * EZ, 256))
    for row in range(EY):
        for slot, fine_z in enumerate(slots):
            if fine_z is None:
                continue
            for y, wy in taps(row - 3):
                for z, wz in taps(fine_z):
                    block[row * EZ + slot, place[y, z]] += wy * wz
    return lines.astype(np.float32), block.astype(np.float32)


def dot(a, b, contract=(1, 0)):
    return lax.dot_general(
        a,
        b,
        (((contract[0],), (contract[1],)), ((), ())),
        precision=HIGH,
        preferred_element_type=jnp.float32,
    )


def spectral_kernel(
    vort,
    scal,
    fwd_x,
    fwd_left,
    twiddle,
    fwd_right,
    waves,
    inv_right,
    inv_left,
    inv_x,
    rim_out,
    ext_out,
    peak_out,
    s_buf,
    r_buf,
    z_buf,
    zo_buf,
    y_buf,
    yo_buf,
    t_buf,
    u_buf,
    pieces,
    peaks,
    peak_row,
    peak_mine,
    peak_other,
    own_sem,
    send_sem,
    recv_sem,
    scal_send,
    scal_recv,
    rim_send,
    rim_recv,
):
    row = lax.axis_index("row")
    col = lax.axis_index("col")
    core = col % 2
    chip = row * 8 + col // 2
    other = 1 - core
    up_row, down_row = (row + 1) % ROWS, (row + ROWS - 1) % ROWS
    up_col, down_col = (col + 1) % COLS, (col + COLS - 1) % COLS

    own = pltpu.make_async_copy(scal, ext_out.at[pl.ds(3, FY), pl.ds(0, FZ), :], own_sem)
    own.start()

    barrier = pltpu.get_barrier_semaphore()

    def greet(i, carry):
        to = (chip + i) % CHIPS
        pl.semaphore_signal(
            barrier, inc=1, device_id=(to // 8, 2 * (to % 8) + other), device_id_type=MESH
        )
        return carry

    lax.fori_loop(0, CHIPS, greet, 0)
    for to_row in (up_row, down_row):
        pl.semaphore_signal(barrier, inc=1, device_id=(to_row, col), device_id_type=MESH)

    for c in range(3):
        s_buf[c] = dot(fwd_x[...], vort[c], (1, 1)).reshape(2, 64, 128)
    pieces[...] = jnp.zeros_like(pieces)
    own.wait()
    pl.semaphore_wait(barrier, CHIPS + 2)

    def exchange(source, target, index):
        def send(i, carry):
            to = (chip + i) % CHIPS
            pltpu.make_async_remote_copy(
                src_ref=source.at[:, :, pl.ds(to, 1), :],
                dst_ref=target.at[:, :, pl.ds(chip, 1), :],
                send_sem=send_sem.at[index],
                recv_sem=recv_sem.at[index],
                device_id=(to // 8, 2 * (to % 8) + other),
                device_id_type=MESH,
            ).start()
            return carry

        lax.fori_loop(0, CHIPS, send, 0)

    def swap(source, target, index):
        pltpu.make_async_remote_copy(
            src_ref=source,
            dst_ref=target,
            send_sem=send_sem.at[index],
            recv_sem=recv_sem.at[index],
            device_id=(row, col + 1 - 2 * core),
            device_id_type=MESH,
        ).start()

    def arrive(target, index):
        pltpu.make_async_copy(target, target, recv_sem.at[index]).wait()

    def left(source, index):
        pltpu.make_async_copy(source, source, send_sem.at[index]).wait()

    exchange(s_buf, r_buf, 0)

    def scal_copy(i, ys, zs, yt, zt, device):
        return pltpu.make_async_remote_copy(
            src_ref=ext_out.at[pl.ds(*ys), pl.ds(*zs), :],
            dst_ref=ext_out.at[pl.ds(*yt), pl.ds(*zt), :],
            send_sem=scal_send.at[i],
            recv_sem=scal_recv.at[i],
            device_id=device,
            device_id_type=MESH,
        )

    y_first, y_last, y_below, y_above, y_all = (3, 3), (32, 3), (0, 3), (35, 3), (3, FY)
    z_first, z_last, z_below, z_above, z_all = (0, 3), (13, 3), (21, 3), (16, 3), (0, FZ)
    scal_copies = [
        scal_copy(0, y_first, z_all, y_above, z_all, (down_row, col)),
        scal_copy(1, y_last, z_all, y_below, z_all, (up_row, col)),
        scal_copy(2, y_all, z_first, y_all, z_above, (row, down_col)),
        scal_copy(3, y_all, z_last, y_all, z_below, (row, up_col)),
        scal_copy(4, y_first, z_first, y_above, z_above, (down_row, down_col)),
        scal_copy(5, y_first, z_last, y_above, z_below, (down_row, up_col)),
        scal_copy(6, y_last, z_first, y_below, z_above, (up_row, down_col)),
        scal_copy(7, y_last, z_last, y_below, z_below, (up_row, up_col)),
    ]
    for copy in scal_copies:
        copy.start()

    arrive(r_buf, 0)
    for c in range(3):
        z_buf[c] = dot(fwd_left[core], r_buf[c].reshape(128, 128))
    swap(z_buf, zo_buf, 1)
    sign = (1 - 2 * core).astype(jnp.float32)
    tw_re = twiddle[core, 0]
    tw_im = twiddle[core, 1]
    ky = waves[core, 0]
    kz = waves[core, 1]
    kx = chip.astype(jnp.float32)
    k_sq = kx * kx + ky * ky + kz * kz
    keep = (k_sq > 0.0) & (ky > -64.0) & (kz > -64.0)
    factor = jnp.where(keep, 1.0 / jnp.maximum(k_sq, 1.0), 0.0) * (1.0 / (N * N * N))
    arrive(zo_buf, 1)
    omega = []
    for c in range(3):
        joined = z_buf[c] + sign * zo_buf[c]
        re, im = joined[:64], joined[64:]
        pair = jnp.concatenate([re * tw_re - im * tw_im, re * tw_im + im * tw_re], axis=1)
        spectrum = dot(pair, fwd_right[...])
        omega.append((spectrum[:, :128], spectrum[:, 128:]))

    def cross(part):
        w0, w1, w2 = omega[0][part], omega[1][part], omega[2][part]
        return (ky * w2 - kz * w1, kz * w0 - kx * w2, kx * w1 - ky * w0)

    cross_re, cross_im = cross(0), cross(1)
    for c in range(3):
        pair = jnp.concatenate([-cross_im[c] * factor, cross_re[c] * factor], axis=1)
        back = dot(pair, inv_right[...])
        re, im = back[:, :128], back[:, 128:]
        y_buf[c, :64] = re * tw_re + im * tw_im
        y_buf[c, 64:] = im * tw_re - re * tw_im
    swap(y_buf, yo_buf, 2)
    arrive(yo_buf, 2)
    for c in range(3):
        joined = y_buf[c] - sign * yo_buf[c]
        t_buf[c] = dot(inv_left[core], joined).reshape(2, 64, 128)
    exchange(t_buf, u_buf, 3)
    arrive(u_buf, 3)
    top = jnp.zeros((8, 128), jnp.float32)
    for c in range(3):
        velocity = dot(u_buf[c].reshape(128, 128), inv_x[...], (0, 0))
        rim_out[c, :128] = velocity
        top = jnp.maximum(top, jnp.max(jnp.abs(velocity).reshape(16, 8, 128), axis=0))
    peak_row[...] = jnp.broadcast_to(jnp.max(top, axis=0, keepdims=True), (8, 128))

    def peak_send(i, carry):
        to = (chip + i) % CHIPS
        pltpu.make_async_remote_copy(
            src_ref=peak_row.at[pl.ds(0, 1), :],
            dst_ref=peaks.at[pl.ds(chip, 1), :],
            send_sem=send_sem.at[4],
            recv_sem=recv_sem.at[4],
            device_id=(to // 8, 2 * (to % 8) + other),
            device_id_type=MESH,
        ).start()
        return carry

    lax.fori_loop(0, CHIPS, peak_send, 0)

    for c in range(3):
        for i in range(2):
            pieces[c, pl.ds(16 * i, 16), :] = rim_out[c, pl.ds(6 + i, 16, 8), :]
            pieces[c, pl.ds(32 + 16 * i, 16), :] = rim_out[c, pl.ds(i, 16, 8), :]
            for index, (y, z) in enumerate(((14, 6), (14, 0), (0, 6), (0, 0))):
                pieces[c, pl.ds(64 + 8 * index + 2 * i, 2), :] = rim_out[
                    c, pl.ds(8 * y + z + i, 2, 8), :
                ]

    def rim_copy(i, source, start, target, count, device):
        return pltpu.make_async_remote_copy(
            src_ref=source.at[:, pl.ds(start, count), :],
            dst_ref=rim_out.at[:, pl.ds(target, count), :],
            send_sem=rim_send.at[i],
            recv_sem=rim_recv.at[i],
            device_id=device,
            device_id_type=MESH,
        )

    rim_copies = [
        rim_copy(0, rim_out, 112, 128, 16, (up_row, col)),
        rim_copy(1, rim_out, 0, 144, 16, (down_row, col)),
        rim_copy(2, pieces, 0, 160, 32, (row, up_col)),
        rim_copy(3, pieces, 32, 192, 32, (row, down_col)),
        rim_copy(4, pieces, 64, 224, 8, (up_row, up_col)),
        rim_copy(5, pieces, 72, 232, 8, (up_row, down_col)),
        rim_copy(6, pieces, 80, 240, 8, (down_row, up_col)),
        rim_copy(7, pieces, 88, 248, 8, (down_row, down_col)),
    ]
    for copy in rim_copies:
        copy.start()
    arrive(peaks, 4)
    peak_mine[...] = jnp.max(peaks[...].reshape(8, 8, 128), axis=0)
    swap(peak_mine, peak_other, 5)
    arrive(peak_other, 5)
    peak_out[...] = jnp.maximum(peak_mine[...], peak_other[...])
    for copy in scal_copies + rim_copies:
        copy.wait_recv()
    left(s_buf, 0)
    left(z_buf, 1)
    left(y_buf, 2)
    left(t_buf, 3)
    left(peaks, 4)
    left(peak_mine, 5)
    for copy in scal_copies + rim_copies:
        copy.wait_send()


def weights(field, moved):
    size = jnp.abs(moved)
    square = moved * moved
    core = square * (7.0 / 48.0 - size * (0.25 - (5.0 / 48.0) * size))
    even = core * size
    odd = core * moved
    near = 2.0 / 3.0 - square * (1.0 / 6.0)
    far = (square - 1.0) * (1.0 / 24.0)
    near_even = square * near + 15.0 * even
    near_odd = moved * near + 5.0 * odd
    far_even = square * far - 6.0 * even
    far_odd = moved * (far + far) - 4.0 * odd
    centre = 1.0 + square * (0.25 * square - 1.25) - 20.0 * even
    return (
        field * (even - odd),
        field * (far_even - far_odd),
        field * (near_even - near_odd),
        field * centre,
        field * (near_even + near_odd),
        field * (far_even + far_odd),
        field * (even + odd),
    )


def sweep_roll(field, moved, axis):
    below3, below2, below1, centre, above1, above2, above3 = weights(field, moved)
    length = field.shape[axis]

    def up(a):
        return pltpu.roll(a, 1, axis)

    def down(a):
        return pltpu.roll(a, length - 1, axis)

    raised = up(above1 + up(above2 + up(above3)))
    lowered = down(below1 + down(below2 + down(below3)))
    return centre + raised + lowered


def remesh_kernel(rim, ext, peak, lines, block, out, moved, swept):
    top = jnp.max(peak[...], axis=1, keepdims=True)
    top = jnp.max(top, axis=0, keepdims=True)
    scale = COURANT / (top + EPSILON)
    for c in range(3):
        wide = dot(rim[c], lines[...]) * scale
        big = wide.astype(jnp.bfloat16)
        small = (wide - big.astype(jnp.float32)).astype(jnp.bfloat16)
        fine = jnp.dot(block[...], big, preferred_element_type=jnp.float32)
        fine = fine + jnp.dot(block[...], small, preferred_element_type=jnp.float32)
        moved[c] = fine.reshape(EY, EZ, 256)

    def along_x(i, carry):
        swept[i] = sweep_roll(ext[i], moved[0, i], 1)
        return carry

    lax.fori_loop(0, EY, along_x, 0)
    for half in range(2):
        lanes = pl.ds(128 * half, 128)

        def along_y(i, held):
            parts = weights(swept[i, :, lanes], moved[1, i, :, lanes])
            held = held + (jnp.zeros((EZ, 128), jnp.float32),)
            held = tuple(a + b for a, b in zip(held, parts))

            @pl.when(i >= 6)
            def _():
                done = sweep_roll(held[0], moved[2, i - 3, :, lanes], 0)
                out[i - 6, :, lanes] = done[:FZ]

            return held[1:]

        lax.fori_loop(0, EY, along_y, (jnp.zeros((EZ, 128), jnp.float32),) * 6)


def shards(vorticity, scalar):
    tables = [jnp.asarray(t) for t in spectral_tables()]
    lines, block = refine_tables()
    vmem = pl.BlockSpec(memory_space=pltpu.VMEM)
    f32 = jnp.float32
    rim, ext, peak = pl.pallas_call(
        spectral_kernel,
        out_shape=(
            jax.ShapeDtypeStruct((3, 256, 128), f32),
            jax.ShapeDtypeStruct((EY, EZ, 256), f32),
            jax.ShapeDtypeStruct((8, 128), f32),
        ),
        in_specs=[vmem, pl.BlockSpec(memory_space=pl.ANY)] + [vmem] * len(tables),
        out_specs=(vmem, vmem, vmem),
        scratch_shapes=[
            pltpu.VMEM((3, 2, 64, 128), f32),
            pltpu.VMEM((3, 2, 64, 128), f32),
            pltpu.VMEM((3, 128, 128), f32),
            pltpu.VMEM((3, 128, 128), f32),
            pltpu.VMEM((3, 128, 128), f32),
            pltpu.VMEM((3, 128, 128), f32),
            pltpu.VMEM((3, 2, 64, 128), f32),
            pltpu.VMEM((3, 2, 64, 128), f32),
            pltpu.VMEM((3, 96, 128), f32),
            pltpu.VMEM((64, 128), f32),
            pltpu.VMEM((8, 128), f32),
            pltpu.VMEM((8, 128), f32),
            pltpu.VMEM((8, 128), f32),
            pltpu.SemaphoreType.DMA,
            pltpu.SemaphoreType.DMA((6,)),
            pltpu.SemaphoreType.DMA((6,)),
            pltpu.SemaphoreType.DMA((8,)),
            pltpu.SemaphoreType.DMA((8,)),
            pltpu.SemaphoreType.DMA((8,)),
            pltpu.SemaphoreType.DMA((8,)),
        ],
        compiler_params=pltpu.CompilerParams(collective_id=0, has_side_effects=True),
        name="spectral",
    )(vorticity.reshape(3, YB * ZB, N), scalar, *tables)
    return pl.pallas_call(
        remesh_kernel,
        out_shape=jax.ShapeDtypeStruct((FY, FZ, 256), f32),
        in_specs=[vmem] * 5,
        out_specs=vmem,
        scratch_shapes=[
            pltpu.VMEM((3, EY, EZ, 256), f32),
            pltpu.VMEM((EY, EZ, 256), f32),
        ],
        name="remesh",
    )(rim, ext, peak, jnp.asarray(lines), jnp.asarray(block, jnp.bfloat16))


def solution(mesh):
    return jax.shard_map(
        shards,
        mesh=mesh,
        in_specs=(P(None, "row", "col", None), P("row", "col", None)),
        out_specs=P("row", "col", None),
        check_vma=False,
    )
```

profile of v0, /device:TPU:1, one launch (start us, length us, event | category | flops | bytes accessed | tf_op | source)
XLA Modules:
  0.0 54.9 jit_solution(9324572887937456533)
XLA Ops:
  0.0 38.0 %spectral.1 = (f32[3,256,128]{2,1,0:T(8,128)}, f32[38,24,256]{2,1,0:T(8,128)}, f32[8,128]{1,0:T(8,128)}) custom-call(f32[3,128,128]{2,1,0:T(8,128)} %bitcast.1, f32[32,16,256]{2,1,0:T(8,128)} %scal.1, f32[128,128]{1,0:T(8,128)} %constant.20.clone.fwd_x, f32[2,128,128]{2,1,0:T(8,128)} %constant.21.clone.fwd_left, f32[2,2,64,128]{3,2,1,0:T(8,128)} %constant.22.clone.twiddle, ...), custom_call_target="tpu_custom_call" | custom-call | tf_op jit(solution)/shard_map/spectral/pallas_call | solution.py:439
  38.1 16.8 %remesh.1 = f32[32,16,256]{2,1,0:T(8,128)} custom-call(f32[3,256,128]{2,1,0:T(8,128)} %get-tuple-element.8.rim, f32[38,24,256]{2,1,0:T(8,128)} %get-tuple-element.9.ext, f32[8,128]{1,0:T(8,128)} %get-tuple-element.10.peak, f32[128,256]{1,0:T(8,128)} %constant.28.clone.lines, bf16[912,256]{1,0:T(8,128)(2,1)} %constant.29.clone.block), custom_call_target="tpu_custom_call" | custom-call | tf_op jit(solution)/shard_map/remesh/pallas_call | solution.py:473
where the time goes:
time: 55 us; the launch traced here: 54.9 us
  Pallas kernels  54.9 us (100%)
    pallas_call x1, Pallas kernels, shards(): pl.pallas_call(spectral_kernel, out_shape=(jax.ShapeDtypeStruct((3, 256,...  38 us
    pallas_call x1, Pallas kernels, shards(): pl.pallas_call(remesh_kernel, out_shape=jax.ShapeDtypeStruct((FY, FZ, 256...  16.8 us

commit v1 on v0

--- a/solution.py
+++ b/solution.py
@@ -11,6 +11,7 @@
 
 COURANT = 0.9
 EPSILON = 1e-06
+VMEM_LIMIT = 24 << 20
 MESH = pl.DeviceIdType.MESH
 HIGH = lax.Precision.HIGH
 
@@ -19,6 +20,7 @@
 CHIPS = 64
 YB, ZB = 16, 8
 FY, FZ = 32, 16
+SLABS = 2
 EY, EZ = 38, 24
 
 
@@ -360,40 +362,35 @@
 def weights(field, moved):
     size = jnp.abs(moved)
     square = moved * moved
-    core = square * (7.0 / 48.0 - size * (0.25 - (5.0 / 48.0) * size))
-    even = core * size
-    odd = core * moved
-    near = 2.0 / 3.0 - square * (1.0 / 6.0)
-    far = (square - 1.0) * (1.0 / 24.0)
-    near_even = square * near + 15.0 * even
-    near_odd = moved * near + 5.0 * odd
-    far_even = square * far - 6.0 * even
-    far_odd = moved * (far + far) - 4.0 * odd
-    centre = 1.0 + square * (0.25 * square - 1.25) - 20.0 * even
+    first = field * moved
+    second = first * moved
+    core = second * (7.0 / 48.0 - size * (0.25 - (5.0 / 48.0) * size))
+    even3 = core * size
+    odd3 = core * moved
+    bend = first * (square * (1.0 / 24.0) - 1.0 / 24.0)
+    even2 = bend * moved - 6.0 * even3
+    odd2 = (bend + bend) - 4.0 * odd3
+    even1 = 0.5 * second - 4.0 * even2 - 9.0 * even3
+    odd1 = 0.5 * first - (odd2 + odd2) - 3.0 * odd3
+    side = even1 + even2 + even3
     return (
-        field * (even - odd),
-        field * (far_even - far_odd),
-        field * (near_even - near_odd),
-        field * centre,
-        field * (near_even + near_odd),
-        field * (far_even + far_odd),
-        field * (even + odd),
+        even3 - odd3,
+        even2 - odd2,
+        even1 - odd1,
+        field - (side + side),
+        even1 + odd1,
+        even2 + odd2,
+        even3 + odd3,
     )
 
 
 def sweep_roll(field, moved, axis):
-    below3, below2, below1, centre, above1, above2, above3 = weights(field, moved)
+    parts = weights(field, moved)
     length = field.shape[axis]
-
-    def up(a):
-        return pltpu.roll(a, 1, axis)
-
-    def down(a):
-        return pltpu.roll(a, length - 1, axis)
-
-    raised = up(above1 + up(above2 + up(above3)))
-    lowered = down(below1 + down(below2 + down(below3)))
-    return centre + raised + lowered
+    total = parts[3]
+    for offset in (-3, -2, -1, 1, 2, 3):
+        total = total + pltpu.roll(parts[3 + offset], offset % length, axis)
+    return total
 
 
 def remesh_kernel(rim, ext, peak, lines, block, out, moved, swept):
@@ -409,10 +406,14 @@
         moved[c] = fine.reshape(EY, EZ, 256)
 
     def along_x(i, carry):
-        swept[i] = sweep_roll(ext[i], moved[0, i], 1)
+        rows = pl.ds(SLABS * i, SLABS)
+        field = ext[rows].reshape(SLABS * EZ, 256)
+        swept[rows] = sweep_roll(field, moved[0, rows].reshape(SLABS * EZ, 256), 1).reshape(
+            SLABS, EZ, 256
+        )
         return carry
 
-    lax.fori_loop(0, EY, along_x, 0)
+    lax.fori_loop(0, EY // SLABS, along_x, 0)
     for half in range(2):
         lanes = pl.ds(128 * half, 128)
 
@@ -443,7 +444,7 @@
             jax.ShapeDtypeStruct((EY, EZ, 256), f32),
             jax.ShapeDtypeStruct((8, 128), f32),
         ),
-        in_specs=[vmem, pl.BlockSpec(memory_space=pl.ANY)] + [vmem] * len(tables),
+        in_specs=[vmem, pl.BlockSpec(memory_space=pltpu.HBM)] + [vmem] * len(tables),
         out_specs=(vmem, vmem, vmem),
         scratch_shapes=[
             pltpu.VMEM((3, 2, 64, 128), f32),
@@ -467,7 +468,7 @@
             pltpu.SemaphoreType.DMA((8,)),
             pltpu.SemaphoreType.DMA((8,)),
         ],
-        compiler_params=pltpu.CompilerParams(collective_id=0, has_side_effects=True),
+        compiler_params=pltpu.CompilerParams(collective_id=0, has_side_effects=True, vmem_limit_bytes=VMEM_LIMIT),
         name="spectral",
     )(vorticity.reshape(3, YB * ZB, N), scalar, *tables)
     return pl.pallas_call(
@@ -479,6 +480,7 @@
             pltpu.VMEM((3, EY, EZ, 256), f32),
             pltpu.VMEM((EY, EZ, 256), f32),
         ],
+        compiler_params=pltpu.CompilerParams(vmem_limit_bytes=VMEM_LIMIT),
         name="remesh",
     )(rim, ext, peak, jnp.asarray(lines), jnp.asarray(block, jnp.bfloat16))
 

time: 55 us -> 54.7 us (level)
  Pallas kernels: 54.9 us -> 45.1 us
  local copies, waits for them, and re-layouts: 0 us -> 9.17 us
    unnamed x0 -> x24, local copies, waits for them, and re-layouts: none -> 9.17 us
    pallas_call x1, Pallas kernels: 16.8 us -> 9.22 us  [shards(): pl.pallas_call(remesh_kernel, out_shape=jax.ShapeDtypeStruct((FY, FZ, 256...]
    pallas_call x1, Pallas kernels: 38 us -> 35.9 us  [shards(): pl.pallas_call(spectral_kernel, out_shape=(jax.ShapeDtypeStruct((3, 256,...]
where the time goes in v1:
time: 54.7 us; the launch traced here: 54.3 us
  Pallas kernels  45.1 us (82%)
  local copies, waits for them, and re-layouts  9.17 us (17%)
    pallas_call x1, Pallas kernels, shards(): pl.pallas_call(spectral_kernel, out_shape=(jax.ShapeDtypeStruct((3, 256,...  35.9 us
    pallas_call x1, Pallas kernels, shards(): pl.pallas_call(remesh_kernel, out_shape=jax.ShapeDtypeStruct((FY, FZ, 256...  9.22 us
    unnamed x24, local copies, waits for them, and re-layouts  9.17 us

profile of v1, /device:TPU:1, one launch (start us, length us, event | category | flops | bytes accessed | tf_op | source)
XLA Modules:
  0.0 54.3 jit_solution(9494007920774529811)
XLA Ops:
  0.0 0.0 copy-start
  0.0 1.0 %copy-done = f32[32,16,256]{2,1,0:T(8,128)S(1)} copy-done((f32[32,16,256]{2,1,0:T(8,128)S(1)}, f32[32,16,256]{2,1,0:T(8,128)}, u32[]{:S(2)}) %copy-start) | copy-done | bytes 524312
  1.0 0.0 copy-start.2
  1.0 0.9 %copy-done.2 = f32[256,256]{1,0:T(8,128)S(1)} copy-done((f32[256,256]{1,0:T(8,128)S(1)}, f32[256,256]{1,0:T(8,128)}, u32[]{:S(2)}) %copy-start.2) | copy-done | bytes 262168
  2.0 0.0 copy-start.3
  2.0 0.9 %copy-done.3 = f32[256,256]{1,0:T(8,128)S(1)} copy-done((f32[256,256]{1,0:T(8,128)S(1)}, f32[256,256]{1,0:T(8,128)}, u32[]{:S(2)}) %copy-start.3) | copy-done | bytes 262168
  2.9 0.0 copy-start.4
  2.9 0.9 %copy-done.4 = f32[3,16,8,128]{3,2,1,0:T(8,128)S(1)} copy-done((f32[3,16,8,128]{3,2,1,0:T(8,128)S(1)}, f32[3,16,8,128]{3,2,1,0:T(8,128)}, u32[]{:S(2)}) %copy-start.4) | copy-done | bytes 196632
  3.9 0.0 copy-start.6
  3.9 0.9 %copy-done.6 = f32[2,128,128]{2,1,0:T(8,128)S(1)} copy-done((f32[2,128,128]{2,1,0:T(8,128)S(1)}, f32[2,128,128]{2,1,0:T(8,128)}, u32[]{:S(2)}) %copy-start.6) | copy-done | bytes 131096
  4.8 0.0 copy-start.7
  4.8 0.9 %copy-done.7 = f32[2,2,64,128]{3,2,1,0:T(8,128)S(1)} copy-done((f32[2,2,64,128]{3,2,1,0:T(8,128)S(1)}, f32[2,2,64,128]{3,2,1,0:T(8,128)}, u32[]{:S(2)}) %copy-start.7) | copy-done | bytes 131096
  5.7 0.0 copy-start.8
  5.7 0.9 %copy-done.8 = f32[2,2,64,128]{3,2,1,0:T(8,128)S(1)} copy-done((f32[2,2,64,128]{3,2,1,0:T(8,128)S(1)}, f32[2,2,64,128]{3,2,1,0:T(8,128)}, u32[]{:S(2)}) %copy-start.8) | copy-done | bytes 131096
  6.6 0.0 copy-start.9
  6.6 0.9 %copy-done.9 = f32[2,128,128]{2,1,0:T(8,128)S(1)} copy-done((f32[2,128,128]{2,1,0:T(8,128)S(1)}, f32[2,128,128]{2,1,0:T(8,128)}, u32[]{:S(2)}) %copy-start.9) | copy-done | bytes 131096
  7.5 0.0 copy-start.10
  7.5 0.8 %copy-done.10 = f32[128,128]{1,0:T(8,128)S(1)} copy-done((f32[128,128]{1,0:T(8,128)S(1)}, f32[128,128]{1,0:T(8,128)}, u32[]{:S(2)}) %copy-start.10) | copy-done | bytes 65560
  8.3 0.0 copy-start.11
  8.3 0.8 %copy-done.11 = f32[128,128]{1,0:T(8,128)S(1)} copy-done((f32[128,128]{1,0:T(8,128)S(1)}, f32[128,128]{1,0:T(8,128)}, u32[]{:S(2)}) %copy-start.11) | copy-done | bytes 65560
  9.2 35.9 %spectral.1 = (f32[3,256,128]{2,1,0:T(8,128)S(1)}, f32[38,24,256]{2,1,0:T(8,128)S(1)}, f32[8,128]{1,0:T(8,128)S(1)}) custom-call(f32[3,128,128]{2,1,0:T(8,128)S(1)} %bitcast.1, f32[32,16,256]{2,1,0:T(8,128)S(1)} %copy-done, f32[128,128]{1,0:T(8,128)S(1)} %copy-done.11, f32[2,128,128]{2,1,0:T(8,128)S(1)} %copy-done.9, f32[2,2,64,128]{3,2,1,0:T(8,128)S(1)} %copy-done.8, ...), custom_call_target="tpu_custom_call" | custom-call | tf_op jit(solution)/shard_map/spectral/pallas_call | solution.py:440
  45.1 0.0 copy-done.1
  45.1 0.0 copy-done.5
  45.1 9.2 %remesh.1 = f32[32,16,256]{2,1,0:T(8,128)} custom-call(f32[3,256,128]{2,1,0:T(8,128)S(1)} %get-tuple-element.8.rim, f32[38,24,256]{2,1,0:T(8,128)S(1)} %get-tuple-element.9.ext, f32[8,128]{1,0:T(8,128)S(1)} %get-tuple-element.10.peak, f32[128,256]{1,0:T(8,128)S(1)} %copy-done.5, bf16[912,256]{1,0:T(8,128)(2,1)S(1)} %copy-done.1), custom_call_target="tpu_custom_call" | custom-call | tf_op jit(solution)/shard_map/remesh/pallas_call | solution.py:474
  (2 shorter events, 0.0 us)
Async XLA Ops:
  0.0 1.0 %copy-start = (f32[32,16,256]{2,1,0:T(8,128)S(1)}, f32[32,16,256]{2,1,0:T(8,128)}, u32[]{:S(2)}) copy-start(f32[32,16,256]{2,1,0:T(8,128)} %scal.1) | copy-start | bytes 1572868
  1.0 0.9 %copy-start.2 = (f32[256,256]{1,0:T(8,128)S(1)}, f32[256,256]{1,0:T(8,128)}, u32[]{:S(2)}) copy-start(f32[256,256]{1,0:T(8,128)} %constant.25.clone.inv_right) | copy-start | bytes 786436
  2.0 0.9 %copy-start.3 = (f32[256,256]{1,0:T(8,128)S(1)}, f32[256,256]{1,0:T(8,128)}, u32[]{:S(2)}) copy-start(f32[256,256]{1,0:T(8,128)} %constant.23.clone.fwd_right) | copy-start | bytes 786436
  2.9 0.9 %copy-start.4 = (f32[3,16,8,128]{3,2,1,0:T(8,128)S(1)}, f32[3,16,8,128]{3,2,1,0:T(8,128)}, u32[]{:S(2)}) copy-start(f32[3,16,8,128]{3,2,1,0:T(8,128)} %param.12) | copy-start | bytes 589828
  3.9 0.9 %copy-start.6 = (f32[2,128,128]{2,1,0:T(8,128)S(1)}, f32[2,128,128]{2,1,0:T(8,128)}, u32[]{:S(2)}) copy-start(f32[2,128,128]{2,1,0:T(8,128)} %constant.26.clone.inv_left) | copy-start | bytes 393220
  4.8 0.9 %copy-start.7 = (f32[2,2,64,128]{3,2,1,0:T(8,128)S(1)}, f32[2,2,64,128]{3,2,1,0:T(8,128)}, u32[]{:S(2)}) copy-start(f32[2,2,64,128]{3,2,1,0:T(8,128)} %constant.24.clone.waves) | copy-start | bytes 393220
  5.7 0.9 %copy-start.8 = (f32[2,2,64,128]{3,2,1,0:T(8,128)S(1)}, f32[2,2,64,128]{3,2,1,0:T(8,128)}, u32[]{:S(2)}) copy-start(f32[2,2,64,128]{3,2,1,0:T(8,128)} %constant.22.clone.twiddle) | copy-start | bytes 393220
  6.6 0.9 %copy-start.9 = (f32[2,128,128]{2,1,0:T(8,128)S(1)}, f32[2,128,128]{2,1,0:T(8,128)}, u32[]{:S(2)}) copy-start(f32[2,128,128]{2,1,0:T(8,128)} %constant.21.clone.fwd_left) | copy-start | bytes 393220
  7.5 0.8 %copy-start.10 = (f32[128,128]{1,0:T(8,128)S(1)}, f32[128,128]{1,0:T(8,128)}, u32[]{:S(2)}) copy-start(f32[128,128]{1,0:T(8,128)} %constant.27.clone.inv_x) | copy-start | bytes 196612
  8.3 0.8 %copy-start.11 = (f32[128,128]{1,0:T(8,128)S(1)}, f32[128,128]{1,0:T(8,128)}, u32[]{:S(2)}) copy-start(f32[128,128]{1,0:T(8,128)} %constant.20.clone.fwd_x) | copy-start | bytes 196612
  9.2 35.9 %copy-start.1 = (bf16[912,256]{1,0:T(8,128)(2,1)S(1)}, bf16[912,256]{1,0:T(8,128)(2,1)}, u32[]{:S(2)}) copy-start(bf16[912,256]{1,0:T(8,128)(2,1)} %constant.29.clone.block) | copy-start | bytes 1400836
  9.2 35.9 %copy-start.5 = (f32[128,256]{1,0:T(8,128)S(1)}, f32[128,256]{1,0:T(8,128)}, u32[]{:S(2)}) copy-start(f32[128,256]{1,0:T(8,128)} %constant.28.clone.lines) | copy-start | bytes 393220

commit v2 on v1

--- a/solution.py
+++ b/solution.py
@@ -127,85 +127,82 @@
     )
 
 
+FAR_FIRST = sorted(
+    ((dx, dy, dz) for dx in range(4) for dy in range(4) for dz in range(4)),
+    key=lambda d: -sum(min(step, 4 - step) for step in d),
+)
+
+
 def spectral_kernel(
-    vort,
+    vort_hbm,
     scal,
-    fwd_x,
-    fwd_left,
-    twiddle,
-    fwd_right,
-    waves,
-    inv_right,
-    inv_left,
-    inv_x,
-    rim_out,
-    ext_out,
-    peak_out,
-    s_buf,
-    r_buf,
-    z_buf,
-    zo_buf,
-    y_buf,
-    yo_buf,
-    t_buf,
-    u_buf,
-    pieces,
-    peaks,
-    peak_row,
-    peak_mine,
-    peak_other,
-    own_sem,
-    send_sem,
-    recv_sem,
-    scal_send,
-    scal_recv,
-    rim_send,
-    rim_recv,
+    *refs,
 ):
+    table_hbm, (rim_out, ext_out, peak_out), refs = refs[:8], refs[8:11], refs[11:]
+    vort, tables, refs = refs[0], refs[1:9], refs[9:]
+    fwd_x, fwd_left, twiddle, fwd_right, waves, inv_right, inv_left, inv_x = tables
+    s_buf, r_buf, z_buf, zo_buf, y_buf, yo_buf, t_buf, u_buf, pieces = refs[:9]
+    peaks, peak_row, peak_mine, peak_other = refs[9:13]
+    load_sem, send_sem, recv_sem, scal_send, scal_recv, rim_send, rim_recv = refs[13:]
+
     row = lax.axis_index("row")
     col = lax.axis_index("col")
-    core = col % 2
-    chip = row * 8 + col // 2
+    core = lax.rem(col, 2)
+    half = lax.div(col, 2)
+    chip = row * 8 + half
     other = 1 - core
-    up_row, down_row = (row + 1) % ROWS, (row + ROWS - 1) % ROWS
-    up_col, down_col = (col + 1) % COLS, (col + COLS - 1) % COLS
-
-    own = pltpu.make_async_copy(scal, ext_out.at[pl.ds(3, FY), pl.ds(0, FZ), :], own_sem)
-    own.start()
+    up_row, down_row = lax.rem(row + 1, ROWS), lax.rem(row + ROWS - 1, ROWS)
+    up_col, down_col = lax.rem(col + 1, COLS), lax.rem(col + COLS - 1, COLS)
+
+    loads = [pltpu.make_async_copy(vort_hbm, vort, load_sem.at[0])]
+    for i in range(8):
+        loads.append(pltpu.make_async_copy(table_hbm[i], tables[i], load_sem.at[1 + i]))
+    loads.append(
+        pltpu.make_async_copy(
+            scal, ext_out.at[pl.ds(3, FY), pl.ds(0, FZ), :], load_sem.at[9]
+        )
+    )
+    for load in loads[:2] + loads[9:] + loads[2:9]:
+        load.start()
+
+    y0, x0 = lax.rem(row, 4), lax.rem(half, 4)
+    z0 = 2 * lax.div(half, 4) + lax.div(row, 4)
+    xs = [lax.rem(x0 + d, 4) for d in range(4)]
+    ys = [lax.rem(y0 + d, 4) for d in range(4)]
+    zs = [lax.rem(z0 + d, 4) for d in range(4)]
+    low = [4 * lax.rem(z, 2) for z in zs]
+    high = [4 * lax.div(z, 2) for z in zs]
+    to_rows = [[low[dz] + ys[dy] for dz in range(4)] for dy in range(4)]
+    to_halves = [[high[dz] + xs[dx] for dz in range(4)] for dx in range(4)]
+    chips = [(to_rows[dy][dz], to_halves[dx][dz]) for dx, dy, dz in FAR_FIRST]
 
     barrier = pltpu.get_barrier_semaphore()
-
-    def greet(i, carry):
-        to = (chip + i) % CHIPS
+    for to_row, to_half in chips:
         pl.semaphore_signal(
-            barrier, inc=1, device_id=(to // 8, 2 * (to % 8) + other), device_id_type=MESH
+            barrier, inc=1, device_id=(to_row, 2 * to_half + other), device_id_type=MESH
         )
-        return carry
-
-    lax.fori_loop(0, CHIPS, greet, 0)
     for to_row in (up_row, down_row):
         pl.semaphore_signal(barrier, inc=1, device_id=(to_row, col), device_id_type=MESH)
 
+    loads[0].wait()
+    loads[1].wait()
     for c in range(3):
         s_buf[c] = dot(fwd_x[...], vort[c], (1, 1)).reshape(2, 64, 128)
     pieces[...] = jnp.zeros_like(pieces)
-    own.wait()
+    for load in loads[2:]:
+        load.wait()
     pl.semaphore_wait(barrier, CHIPS + 2)
 
     def exchange(source, target, index):
-        def send(i, carry):
-            to = (chip + i) % CHIPS
+        for to_row, to_half in chips:
             pltpu.make_async_remote_copy(
-                src_ref=source.at[:, :, pl.ds(to, 1), :],
+                src_ref=source.at[:, :, pl.ds(to_row * 8 + to_half, 1), :],
                 dst_ref=target.at[:, :, pl.ds(chip, 1), :],
                 send_sem=send_sem.at[index],
                 recv_sem=recv_sem.at[index],
-                device_id=(to // 8, 2 * (to % 8) + other),
+                device_id=(to_row, 2 * to_half + other),
                 device_id_type=MESH,
             ).start()
-            return carry
-
-        lax.fori_loop(0, CHIPS, send, 0)
 
     def swap(source, target, index):
         pltpu.make_async_remote_copy(
@@ -297,19 +294,15 @@
         top = jnp.maximum(top, jnp.max(jnp.abs(velocity).reshape(16, 8, 128), axis=0))
     peak_row[...] = jnp.broadcast_to(jnp.max(top, axis=0, keepdims=True), (8, 128))
 
-    def peak_send(i, carry):
-        to = (chip + i) % CHIPS
+    for to_row, to_half in chips:
         pltpu.make_async_remote_copy(
             src_ref=peak_row.at[pl.ds(0, 1), :],
             dst_ref=peaks.at[pl.ds(chip, 1), :],
             send_sem=send_sem.at[4],
             recv_sem=recv_sem.at[4],
-            device_id=(to // 8, 2 * (to % 8) + other),
+            device_id=(to_row, 2 * to_half + other),
             device_id_type=MESH,
         ).start()
-        return carry
-
-    lax.fori_loop(0, CHIPS, peak_send, 0)
 
     for c in range(3):
         for i in range(2):
@@ -437,16 +430,19 @@
     lines, block = refine_tables()
     vmem = pl.BlockSpec(memory_space=pltpu.VMEM)
     f32 = jnp.float32
+    operands = [vorticity.reshape(3, YB * ZB, N), scalar] + tables
     rim, ext, peak = pl.pallas_call(
         spectral_kernel,
         out_shape=(
-            jax.ShapeDtypeStruct((3, 256, 128), f32),
-            jax.ShapeDtypeStruct((EY, EZ, 256), f32),
-            jax.ShapeDtypeStruct((8, 128), f32),
+            pltpu.VMEM((3, 256, 128), f32),
+            pltpu.VMEM((EY, EZ, 256), f32),
+            pltpu.VMEM((8, 128), f32),
         ),
-        in_specs=[vmem, pl.BlockSpec(memory_space=pltpu.HBM)] + [vmem] * len(tables),
+        in_specs=[pl.BlockSpec(memory_space=pltpu.HBM)] * len(operands),
         out_specs=(vmem, vmem, vmem),
         scratch_shapes=[
+            pltpu.VMEM((3, 128, 128), f32),
+            *[pltpu.VMEM(t.shape, f32) for t in tables],
             pltpu.VMEM((3, 2, 64, 128), f32),
             pltpu.VMEM((3, 2, 64, 128), f32),
             pltpu.VMEM((3, 128, 128), f32),
@@ -460,7 +456,7 @@
             pltpu.VMEM((8, 128), f32),
             pltpu.VMEM((8, 128), f32),
             pltpu.VMEM((8, 128), f32),
-            pltpu.SemaphoreType.DMA,
+            pltpu.SemaphoreType.DMA((10,)),
             pltpu.SemaphoreType.DMA((6,)),
             pltpu.SemaphoreType.DMA((6,)),
             pltpu.SemaphoreType.DMA((8,)),
@@ -470,7 +466,7 @@
         ],
         compiler_params=pltpu.CompilerParams(collective_id=0, has_side_effects=True, vmem_limit_bytes=VMEM_LIMIT),
         name="spectral",
-    )(vorticity.reshape(3, YB * ZB, N), scalar, *tables)
+    )(*[pltpu.with_memory_space_constraint(a, pltpu.HBM) for a in operands])
     return pl.pallas_call(
         remesh_kernel,
         out_shape=jax.ShapeDtypeStruct((FY, FZ, 256), f32),

time: 54.7 us -> 42.7 us (0.78)
  local copies, waits for them, and re-layouts: 9.17 us -> 0.01 us
  Pallas kernels: 45.1 us -> 42.5 us
    unnamed x24 -> x4, local copies, waits for them, and re-layouts: 9.17 us -> 0.01 us
    pallas_call x1, Pallas kernels: 35.9 us -> 33.3 us  [shards(): pl.pallas_call(spectral_kernel, out_shape=(pltpu.VMEM((3, 256, 128), f32)...]
where the time goes in v2:
time: 42.7 us; the launch traced here: 42.6 us
  Pallas kernels  42.5 us (100%)
    pallas_call x1, Pallas kernels, shards(): pl.pallas_call(spectral_kernel, out_shape=(pltpu.VMEM((3, 256, 128), f32)...  33.3 us
    pallas_call x1, Pallas kernels, shards(): pl.pallas_call(remesh_kernel, out_shape=jax.ShapeDtypeStruct((FY, FZ, 256...  9.21 us

profile of v2, /device:TPU:1, one launch (start us, length us, event | category | flops | bytes accessed | tf_op | source)
XLA Modules:
  0.0 42.6 jit_solution(3778054307922608385)
XLA Ops:
  0.0 0.0 copy-start
  0.0 0.0 copy-start.1
  0.0 33.3 %spectral.1 = (f32[3,256,128]{2,1,0:T(8,128)S(1)}, f32[38,24,256]{2,1,0:T(8,128)S(1)}, f32[8,128]{1,0:T(8,128)S(1)}) custom-call(f32[3,128,128]{2,1,0:T(8,128)} %bitcast.1, f32[32,16,256]{2,1,0:T(8,128)} %scal.1, f32[128,128]{1,0:T(8,128)} %constant.20.clone.refs_0_, f32[2,128,128]{2,1,0:T(8,128)} %constant.21.clone.refs_1_, ...), custom_call_target="tpu_custom_call" | custom-call | tf_op jit(solution)/shard_map/spectral/pallas_call | solution.py:434
  33.3 0.0 copy-done
  33.4 0.0 copy-done.1
  33.4 9.2 %remesh.1 = f32[32,16,256]{2,1,0:T(8,128)} custom-call(f32[3,256,128]{2,1,0:T(8,128)S(1)} %get-tuple-element.8.rim, f32[38,24,256]{2,1,0:T(8,128)S(1)} %get-tuple-element.9.ext, f32[8,128]{1,0:T(8,128)S(1)} %get-tuple-element.10.peak, f32[128,256]{1,0:T(8,128)S(1)} %copy-done.1, bf16[912,256]{1,0:T(8,128)(2,1)S(1)} %copy-done), custom_call_target="tpu_custom_call" | custom-call | tf_op jit(solution)/shard_map/remesh/pallas_call | solution.py:470
Async XLA Ops:
  0.0 33.3 %copy-start = (bf16[912,256]{1,0:T(8,128)(2,1)S(1)}, bf16[912,256]{1,0:T(8,128)(2,1)}, u32[]{:S(2)}) copy-start(bf16[912,256]{1,0:T(8,128)(2,1)} %constant.29.clone.block) | copy-start | bytes 1400836
  0.0 33.4 %copy-start.1 = (f32[128,256]{1,0:T(8,128)S(1)}, f32[128,256]{1,0:T(8,128)}, u32[]{:S(2)}) copy-start(f32[128,256]{1,0:T(8,128)} %constant.28.clone.lines) | copy-start | bytes 393220

commit v3 on v2

--- a/solution.py
+++ b/solution.py
@@ -20,7 +20,7 @@
 CHIPS = 64
 YB, ZB = 16, 8
 FY, FZ = 32, 16
-SLABS = 2
+STEP = 19
 EY, EZ = 38, 24
 
 
@@ -138,12 +138,11 @@
     scal,
     *refs,
 ):
-    table_hbm, (rim_out, ext_out, peak_out), refs = refs[:8], refs[8:11], refs[11:]
-    vort, tables, refs = refs[0], refs[1:9], refs[9:]
-    fwd_x, fwd_left, twiddle, fwd_right, waves, inv_right, inv_left, inv_x = tables
-    s_buf, r_buf, z_buf, zo_buf, y_buf, yo_buf, t_buf, u_buf, pieces = refs[:9]
-    peaks, peak_row, peak_mine, peak_other = refs[9:13]
-    load_sem, send_sem, recv_sem, scal_send, scal_recv, rim_send, rim_recv = refs[13:]
+    table_hbm, (moved_out, ext_out, peak_out), refs = refs[:10], refs[10:13], refs[13:]
+    vort, tables, refs = refs[0], refs[1:11], refs[11:]
+    fwd_x, fwd_left, twiddle, fwd_right, waves, inv_right, inv_left, inv_x, lines, block = tables
+    s_buf, r_buf, z_buf, zo_buf, y_buf, yo_buf, t_buf, u_buf, rim, pieces, peaks = refs[:11]
+    load_sem, send_sem, recv_sem, scal_send, scal_recv, rim_send, rim_recv = refs[11:]
 
     row = lax.axis_index("row")
     col = lax.axis_index("col")
@@ -155,14 +154,14 @@
     up_col, down_col = lax.rem(col + 1, COLS), lax.rem(col + COLS - 1, COLS)
 
     loads = [pltpu.make_async_copy(vort_hbm, vort, load_sem.at[0])]
-    for i in range(8):
+    for i in range(10):
         loads.append(pltpu.make_async_copy(table_hbm[i], tables[i], load_sem.at[1 + i]))
     loads.append(
         pltpu.make_async_copy(
-            scal, ext_out.at[pl.ds(3, FY), pl.ds(0, FZ), :], load_sem.at[9]
+            scal, ext_out.at[pl.ds(3, FY), pl.ds(0, FZ), :], load_sem.at[11]
         )
     )
-    for load in loads[:2] + loads[9:] + loads[2:9]:
+    for load in loads[:2] + loads[11:] + loads[2:11]:
         load.start()
 
     y0, x0 = lax.rem(row, 4), lax.rem(half, 4)
@@ -181,8 +180,10 @@
         pl.semaphore_signal(
             barrier, inc=1, device_id=(to_row, 2 * to_half + other), device_id_type=MESH
         )
-    for to_row in (up_row, down_row):
-        pl.semaphore_signal(barrier, inc=1, device_id=(to_row, col), device_id_type=MESH)
+    for to_row, to_half in chips[:-1]:
+        pl.semaphore_signal(
+            barrier, inc=1, device_id=(to_row, 2 * to_half + core), device_id_type=MESH
+        )
 
     loads[0].wait()
     loads[1].wait()
@@ -191,7 +192,7 @@
     pieces[...] = jnp.zeros_like(pieces)
     for load in loads[2:]:
         load.wait()
-    pl.semaphore_wait(barrier, CHIPS + 2)
+    pl.semaphore_wait(barrier, 2 * CHIPS - 1)
 
     def exchange(source, target, index):
         for to_row, to_half in chips:
@@ -290,33 +291,34 @@
     top = jnp.zeros((8, 128), jnp.float32)
     for c in range(3):
         velocity = dot(u_buf[c].reshape(128, 128), inv_x[...], (0, 0))
-        rim_out[c, :128] = velocity
+        rim[c, :128] = velocity
         top = jnp.maximum(top, jnp.max(jnp.abs(velocity).reshape(16, 8, 128), axis=0))
-    peak_row[...] = jnp.broadcast_to(jnp.max(top, axis=0, keepdims=True), (8, 128))
-
-    for to_row, to_half in chips:
-        pltpu.make_async_remote_copy(
-            src_ref=peak_row.at[pl.ds(0, 1), :],
-            dst_ref=peaks.at[pl.ds(chip, 1), :],
-            send_sem=send_sem.at[4],
-            recv_sem=recv_sem.at[4],
-            device_id=(to_row, 2 * to_half + other),
-            device_id_type=MESH,
-        ).start()
+    mine = row * COLS + col
+    peaks[pl.ds(mine, 1), :] = jnp.max(top, axis=0, keepdims=True)
+    for to_core, targets in ((other, chips), (core, chips[:-1])):
+        for to_row, to_half in targets:
+            pltpu.make_async_remote_copy(
+                src_ref=peaks.at[pl.ds(mine, 1), :],
+                dst_ref=peaks.at[pl.ds(mine, 1), :],
+                send_sem=send_sem.at[4],
+                recv_sem=recv_sem.at[4],
+                device_id=(to_row, 2 * to_half + to_core),
+                device_id_type=MESH,
+            ).start()
 
     for c in range(3):
         for i in range(2):
-            pieces[c, pl.ds(16 * i, 16), :] = rim_out[c, pl.ds(6 + i, 16, 8), :]
-            pieces[c, pl.ds(32 + 16 * i, 16), :] = rim_out[c, pl.ds(i, 16, 8), :]
+            pieces[c, pl.ds(16 * i, 16), :] = rim[c, pl.ds(6 + i, 16, 8), :]
+            pieces[c, pl.ds(32 + 16 * i, 16), :] = rim[c, pl.ds(i, 16, 8), :]
             for index, (y, z) in enumerate(((14, 6), (14, 0), (0, 6), (0, 0))):
-                pieces[c, pl.ds(64 + 8 * index + 2 * i, 2), :] = rim_out[
+                pieces[c, pl.ds(64 + 8 * index + 2 * i, 2), :] = rim[
                     c, pl.ds(8 * y + z + i, 2, 8), :
                 ]
 
     def rim_copy(i, source, start, target, count, device):
         return pltpu.make_async_remote_copy(
             src_ref=source.at[:, pl.ds(start, count), :],
-            dst_ref=rim_out.at[:, pl.ds(target, count), :],
+            dst_ref=rim.at[:, pl.ds(target, count), :],
             send_sem=rim_send.at[i],
             recv_sem=rim_recv.at[i],
             device_id=device,
@@ -324,8 +326,8 @@
         )
 
     rim_copies = [
-        rim_copy(0, rim_out, 112, 128, 16, (up_row, col)),
-        rim_copy(1, rim_out, 0, 144, 16, (down_row, col)),
+        rim_copy(0, rim, 112, 128, 16, (up_row, col)),
+        rim_copy(1, rim, 0, 144, 16, (down_row, col)),
         rim_copy(2, pieces, 0, 160, 32, (row, up_col)),
         rim_copy(3, pieces, 32, 192, 32, (row, down_col)),
         rim_copy(4, pieces, 64, 224, 8, (up_row, up_col)),
@@ -335,19 +337,25 @@
     ]
     for copy in rim_copies:
         copy.start()
-    arrive(peaks, 4)
-    peak_mine[...] = jnp.max(peaks[...].reshape(8, 8, 128), axis=0)
-    swap(peak_mine, peak_other, 5)
-    arrive(peak_other, 5)
-    peak_out[...] = jnp.maximum(peak_mine[...], peak_other[...])
-    for copy in scal_copies + rim_copies:
+    for copy in rim_copies:
+        copy.wait_recv()
+    for c in range(3):
+        wide = dot(rim[c], lines[...])
+        big = wide.astype(jnp.bfloat16)
+        small = (wide - big.astype(jnp.float32)).astype(jnp.bfloat16)
+        fine = jnp.dot(block[...], big, preferred_element_type=jnp.float32)
+        fine = fine + jnp.dot(block[...], small, preferred_element_type=jnp.float32)
+        moved_out[c] = fine.reshape(EY, EZ, 256)
+    others = peaks.at[pl.ds(0, 2 * CHIPS - 1), :]
+    arrive(others, 4)
+    peak_out[...] = jnp.max(peaks[...].reshape(16, 8, 128), axis=0)
+    for copy in scal_copies:
         copy.wait_recv()
     left(s_buf, 0)
     left(z_buf, 1)
     left(y_buf, 2)
     left(t_buf, 3)
-    left(peaks, 4)
-    left(peak_mine, 5)
+    left(others, 4)
     for copy in scal_copies + rim_copies:
         copy.wait_send()
 
@@ -386,55 +394,71 @@
     return total
 
 
-def remesh_kernel(rim, ext, peak, lines, block, out, moved, swept):
+def remesh_kernel(moved, ext, peak, out, swept, landed, shifts):
     top = jnp.max(peak[...], axis=1, keepdims=True)
     top = jnp.max(top, axis=0, keepdims=True)
     scale = COURANT / (top + EPSILON)
-    for c in range(3):
-        wide = dot(rim[c], lines[...]) * scale
-        big = wide.astype(jnp.bfloat16)
-        small = (wide - big.astype(jnp.float32)).astype(jnp.bfloat16)
-        fine = jnp.dot(block[...], big, preferred_element_type=jnp.float32)
-        fine = fine + jnp.dot(block[...], small, preferred_element_type=jnp.float32)
-        moved[c] = fine.reshape(EY, EZ, 256)
 
     def along_x(i, carry):
-        rows = pl.ds(SLABS * i, SLABS)
-        field = ext[rows].reshape(SLABS * EZ, 256)
-        swept[rows] = sweep_roll(field, moved[0, rows].reshape(SLABS * EZ, 256), 1).reshape(
-            SLABS, EZ, 256
-        )
+        for tile in range(STEP):
+            rows = pl.ds(pl.multiple_of(8 * (STEP * i + tile), 8), 8)
+            total = sweep_roll(ext[rows], scale * moved[0, rows], 1)
+            swept[0, rows] = total[:, :128]
+            swept[1, rows] = total[:, 128:]
         return carry
 
-    lax.fori_loop(0, EY // SLABS, along_x, 0)
+    lax.fori_loop(0, EY * EZ // 8 // STEP, along_x, 0)
     for half in range(2):
         lanes = pl.ds(128 * half, 128)
 
-        def along_y(i, held):
-            parts = weights(swept[i, :, lanes], moved[1, i, :, lanes])
-            held = held + (jnp.zeros((EZ, 128), jnp.float32),)
-            held = tuple(a + b for a, b in zip(held, parts))
-
-            @pl.when(i >= 6)
-            def _():
-                done = sweep_roll(held[0], moved[2, i - 3, :, lanes], 0)
-                out[i - 6, :, lanes] = done[:FZ]
-
-            return held[1:]
-
-        lax.fori_loop(0, EY, along_y, (jnp.zeros((EZ, 128), jnp.float32),) * 6)
+        def along_y(tile, carry):
+            held = [None] * EY
+            for y in range(EY):
+                rows = pl.ds(pl.multiple_of(8 * tile + EZ * y, 8), 8)
+                parts = weights(swept[half, rows], scale * moved[1, rows, lanes])
+                for target in range(max(y - 6, 0), min(y + 1, FY)):
+                    part = parts[target - y + 6]
+                    held[target] = part if held[target] is None else held[target] + part
+                if y >= 6:
+                    slots = pl.ds(pl.multiple_of(8 * tile + EZ * (y - 6), 8), 8)
+                    landed[half, slots] = held[y - 6]
+            return carry
+
+        lax.fori_loop(0, EZ // 8, along_y, 0)
+
+    def along_z(y, carry):
+        for half in range(2):
+            lanes = pl.ds(128 * half, 128)
+            here = pl.ds(pl.multiple_of(EZ * y, 8), EZ)
+            there = pl.ds(pl.multiple_of(EZ * (y + 3), 8), EZ)
+            parts = weights(landed[half, here], scale * moved[2, there, lanes])
+            total = parts[3][:FZ]
+            for k, offset in enumerate((-3, -2, -1, 1, 2, 3)):
+                part = parts[3 + offset]
+                room = shifts.at[half, k]
+                room[8:24, :] = part[:FZ]
+                if offset > 0:
+                    room[0:8, :] = part[FZ:]
+                else:
+                    room[24:32, :] = part[FZ:]
+                total = total + room[pl.ds(8 - offset, FZ), :]
+            out[y, :, lanes] = total
+        return carry
+
+    lax.fori_loop(0, FY, along_z, 0)
 
 
 def shards(vorticity, scalar):
-    tables = [jnp.asarray(t) for t in spectral_tables()]
     lines, block = refine_tables()
+    tables = [jnp.asarray(t) for t in spectral_tables() + (lines,)]
+    tables.append(jnp.asarray(block, jnp.bfloat16))
     vmem = pl.BlockSpec(memory_space=pltpu.VMEM)
     f32 = jnp.float32
     operands = [vorticity.reshape(3, YB * ZB, N), scalar] + tables
-    rim, ext, peak = pl.pallas_call(
+    moved, ext, peak = pl.pallas_call(
         spectral_kernel,
         out_shape=(
-            pltpu.VMEM((3, 256, 128), f32),
+            pltpu.VMEM((3, EY, EZ, 256), f32),
             pltpu.VMEM((EY, EZ, 256), f32),
             pltpu.VMEM((8, 128), f32),
         ),
@@ -442,7 +466,7 @@
         out_specs=(vmem, vmem, vmem),
         scratch_shapes=[
             pltpu.VMEM((3, 128, 128), f32),
-            *[pltpu.VMEM(t.shape, f32) for t in tables],
+            *[pltpu.VMEM(t.shape, t.dtype) for t in tables],
             pltpu.VMEM((3, 2, 64, 128), f32),
             pltpu.VMEM((3, 2, 64, 128), f32),
             pltpu.VMEM((3, 128, 128), f32),
@@ -451,34 +475,35 @@
             pltpu.VMEM((3, 128, 128), f32),
             pltpu.VMEM((3, 2, 64, 128), f32),
             pltpu.VMEM((3, 2, 64, 128), f32),
+            pltpu.VMEM((3, 256, 128), f32),
             pltpu.VMEM((3, 96, 128), f32),
-            pltpu.VMEM((64, 128), f32),
-            pltpu.VMEM((8, 128), f32),
-            pltpu.VMEM((8, 128), f32),
-            pltpu.VMEM((8, 128), f32),
-            pltpu.SemaphoreType.DMA((10,)),
-            pltpu.SemaphoreType.DMA((6,)),
-            pltpu.SemaphoreType.DMA((6,)),
+            pltpu.VMEM((128, 128), f32),
+            pltpu.SemaphoreType.DMA((12,)),
+            pltpu.SemaphoreType.DMA((5,)),
+            pltpu.SemaphoreType.DMA((5,)),
             pltpu.SemaphoreType.DMA((8,)),
             pltpu.SemaphoreType.DMA((8,)),
             pltpu.SemaphoreType.DMA((8,)),
             pltpu.SemaphoreType.DMA((8,)),
         ],
-        compiler_params=pltpu.CompilerParams(collective_id=0, has_side_effects=True, vmem_limit_bytes=VMEM_LIMIT),
+        compiler_params=pltpu.CompilerParams(
+            collective_id=0, has_side_effects=True, vmem_limit_bytes=VMEM_LIMIT
+        ),
         name="spectral",
     )(*[pltpu.with_memory_space_constraint(a, pltpu.HBM) for a in operands])
     return pl.pallas_call(
         remesh_kernel,
         out_shape=jax.ShapeDtypeStruct((FY, FZ, 256), f32),
-        in_specs=[vmem] * 5,
+        in_specs=[vmem] * 3,
         out_specs=vmem,
         scratch_shapes=[
-            pltpu.VMEM((3, EY, EZ, 256), f32),
-            pltpu.VMEM((EY, EZ, 256), f32),
+            pltpu.VMEM((2, EY * EZ, 128), f32),
+            pltpu.VMEM((2, FY * EZ, 128), f32),
+            pltpu.VMEM((2, 6, 32, 128), f32),
         ],
         compiler_params=pltpu.CompilerParams(vmem_limit_bytes=VMEM_LIMIT),
         name="remesh",
-    )(rim, ext, peak, jnp.asarray(lines), jnp.asarray(block, jnp.bfloat16))
+    )(moved.reshape(3, EY * EZ, 256), ext.reshape(EY * EZ, 256), peak)
 
 
 def solution(mesh):

time: 42.7 us -> 39.4 us (0.923)
  Pallas kernels: 42.5 us -> 39.1 us
    pallas_call x1, Pallas kernels: 9.21 us -> 6 us  [shards(): pl.pallas_call(remesh_kernel, out_shape=jax.ShapeDtypeStruct((FY, FZ, 256...]
where the time goes in v3:
time: 39.4 us; the launch traced here: 39.1 us
  Pallas kernels  39.1 us (99%)
    pallas_call x1, Pallas kernels, shards(): pl.pallas_call(spectral_kernel, out_shape=(pltpu.VMEM((3, EY, EZ, 256), f...  33.1 us
    pallas_call x1, Pallas kernels, shards(): pl.pallas_call(remesh_kernel, out_shape=jax.ShapeDtypeStruct((FY, FZ, 256...  6 us

profile of v3, /device:TPU:1, one launch (start us, length us, event | category | flops | bytes accessed | tf_op | source)
XLA Modules:
  0.0 39.1 jit_solution(16289952792613541737)
XLA Ops:
  0.0 33.1 %spectral.1 = (f32[3,38,24,256]{3,2,1,0:T(8,128)S(1)}, f32[38,24,256]{2,1,0:T(8,128)S(1)}, f32[8,128]{1,0:T(8,128)S(1)}) custom-call(f32[3,128,128]{2,1,0:T(8,128)} %bitcast.5, f32[32,16,256]{2,1,0:T(8,128)} %scal.1, f32[128,128]{1,0:T(8,128)} %constant.20.clone.refs_0_, f32[2,128,128]{2,1,0:T(8,128)} %constant.21.clone.refs_1_, ...), custom_call_target="tpu_custom_call" | custom-call | tf_op jit(solution)/shard_map/spectral/pallas_call | solution.py:458
  33.1 6.0 %remesh.1 = f32[32,16,256]{2,1,0:T(8,128)} custom-call(f32[3,912,256]{2,1,0:T(8,128)S(1)} %bitcast.3, f32[912,256]{1,0:T(8,128)S(1)} %bitcast.4, f32[8,128]{1,0:T(8,128)S(1)} %get-tuple-element.10.peak), custom_call_target="tpu_custom_call" | custom-call | tf_op jit(solution)/shard_map/remesh/pallas_call | solution.py:494

commit v4 on v3

--- a/solution.py
+++ b/solution.py
@@ -138,11 +138,12 @@
     scal,
     *refs,
 ):
-    table_hbm, (moved_out, ext_out, peak_out), refs = refs[:10], refs[10:13], refs[13:]
+    table_hbm, (moved_out, wide_out, ext_out, peak_out), refs = refs[:10], refs[10:14], refs[14:]
     vort, tables, refs = refs[0], refs[1:11], refs[11:]
     fwd_x, fwd_left, twiddle, fwd_right, waves, inv_right, inv_left, inv_x, lines, block = tables
     s_buf, r_buf, z_buf, zo_buf, y_buf, yo_buf, t_buf, u_buf, rim, pieces, peaks = refs[:11]
-    load_sem, send_sem, recv_sem, scal_send, scal_recv, rim_send, rim_recv = refs[11:]
+    load_sem, send_sem, recv_sem, swap_send, swap_recv = refs[11:16]
+    scal_send, scal_recv, rim_send, rim_recv = refs[16:]
 
     row = lax.axis_index("row")
     col = lax.axis_index("col")
@@ -174,16 +175,11 @@
     to_rows = [[low[dz] + ys[dy] for dz in range(4)] for dy in range(4)]
     to_halves = [[high[dz] + xs[dx] for dz in range(4)] for dx in range(4)]
     chips = [(to_rows[dy][dz], to_halves[dx][dz]) for dx, dy, dz in FAR_FIRST]
+    devices = [(r, 2 * h + c) for r, h in chips for c in (other, core)][:-1]
 
     barrier = pltpu.get_barrier_semaphore()
-    for to_row, to_half in chips:
-        pl.semaphore_signal(
-            barrier, inc=1, device_id=(to_row, 2 * to_half + other), device_id_type=MESH
-        )
-    for to_row, to_half in chips[:-1]:
-        pl.semaphore_signal(
-            barrier, inc=1, device_id=(to_row, 2 * to_half + core), device_id_type=MESH
-        )
+    for device in devices:
+        pl.semaphore_signal(barrier, inc=1, device_id=device, device_id_type=MESH)
 
     loads[0].wait()
     loads[1].wait()
@@ -205,15 +201,17 @@
                 device_id_type=MESH,
             ).start()
 
-    def swap(source, target, index):
-        pltpu.make_async_remote_copy(
-            src_ref=source,
-            dst_ref=target,
-            send_sem=send_sem.at[index],
-            recv_sem=recv_sem.at[index],
+    def swap(source, target, index, c):
+        copy = pltpu.make_async_remote_copy(
+            src_ref=source.at[c],
+            dst_ref=target.at[c],
+            send_sem=swap_send.at[index, c],
+            recv_sem=swap_recv.at[index, c],
             device_id=(row, col + 1 - 2 * core),
             device_id_type=MESH,
-        ).start()
+        )
+        copy.start()
+        return copy
 
     def arrive(target, index):
         pltpu.make_async_copy(target, target, recv_sem.at[index]).wait()
@@ -249,9 +247,10 @@
         copy.start()
 
     arrive(r_buf, 0)
+    swaps = []
     for c in range(3):
         z_buf[c] = dot(fwd_left[core], r_buf[c].reshape(128, 128))
-    swap(z_buf, zo_buf, 1)
+        swaps.append(swap(z_buf, zo_buf, 0, c))
     sign = (1 - 2 * core).astype(jnp.float32)
     tw_re = twiddle[core, 0]
     tw_im = twiddle[core, 1]
@@ -261,9 +260,9 @@
     k_sq = kx * kx + ky * ky + kz * kz
     keep = (k_sq > 0.0) & (ky > -64.0) & (kz > -64.0)
     factor = jnp.where(keep, 1.0 / jnp.maximum(k_sq, 1.0), 0.0) * (1.0 / (N * N * N))
-    arrive(zo_buf, 1)
     omega = []
     for c in range(3):
+        swaps[c].wait_recv()
         joined = z_buf[c] + sign * zo_buf[c]
         re, im = joined[:64], joined[64:]
         pair = jnp.concatenate([re * tw_re - im * tw_im, re * tw_im + im * tw_re], axis=1)
@@ -281,13 +280,13 @@
         re, im = back[:, :128], back[:, 128:]
         y_buf[c, :64] = re * tw_re + im * tw_im
         y_buf[c, 64:] = im * tw_re - re * tw_im
-    swap(y_buf, yo_buf, 2)
-    arrive(yo_buf, 2)
-    for c in range(3):
+        swaps.append(swap(y_buf, yo_buf, 1, c))
+    for c in range(3):
+        swaps[3 + c].wait_recv()
         joined = y_buf[c] - sign * yo_buf[c]
         t_buf[c] = dot(inv_left[core], joined).reshape(2, 64, 128)
-    exchange(t_buf, u_buf, 3)
-    arrive(u_buf, 3)
+    exchange(t_buf, u_buf, 1)
+    arrive(u_buf, 1)
     top = jnp.zeros((8, 128), jnp.float32)
     for c in range(3):
         velocity = dot(u_buf[c].reshape(128, 128), inv_x[...], (0, 0))
@@ -295,17 +294,6 @@
         top = jnp.maximum(top, jnp.max(jnp.abs(velocity).reshape(16, 8, 128), axis=0))
     mine = row * COLS + col
     peaks[pl.ds(mine, 1), :] = jnp.max(top, axis=0, keepdims=True)
-    for to_core, targets in ((other, chips), (core, chips[:-1])):
-        for to_row, to_half in targets:
-            pltpu.make_async_remote_copy(
-                src_ref=peaks.at[pl.ds(mine, 1), :],
-                dst_ref=peaks.at[pl.ds(mine, 1), :],
-                send_sem=send_sem.at[4],
-                recv_sem=recv_sem.at[4],
-                device_id=(to_row, 2 * to_half + to_core),
-                device_id_type=MESH,
-            ).start()
-
     for c in range(3):
         for i in range(2):
             pieces[c, pl.ds(16 * i, 16), :] = rim[c, pl.ds(6 + i, 16, 8), :]
@@ -337,27 +325,41 @@
     ]
     for copy in rim_copies:
         copy.start()
+    for device in devices:
+        pltpu.make_async_remote_copy(
+            src_ref=peaks.at[pl.ds(mine, 1), :],
+            dst_ref=peaks.at[pl.ds(mine, 1), :],
+            send_sem=send_sem.at[2],
+            recv_sem=recv_sem.at[2],
+            device_id=device,
+            device_id_type=MESH,
+        ).start()
     for copy in rim_copies:
         copy.wait_recv()
     for c in range(3):
         wide = dot(rim[c], lines[...])
         big = wide.astype(jnp.bfloat16)
         small = (wide - big.astype(jnp.float32)).astype(jnp.bfloat16)
-        fine = jnp.dot(block[...], big, preferred_element_type=jnp.float32)
-        fine = fine + jnp.dot(block[...], small, preferred_element_type=jnp.float32)
-        moved_out[c] = fine.reshape(EY, EZ, 256)
+        if c == 0:
+            moved_out[...] = refine(block[...], big, small)
+        else:
+            wide_out[2 * c - 2] = big
+            wide_out[2 * c - 1] = small
     others = peaks.at[pl.ds(0, 2 * CHIPS - 1), :]
-    arrive(others, 4)
+    arrive(others, 2)
     peak_out[...] = jnp.max(peaks[...].reshape(16, 8, 128), axis=0)
     for copy in scal_copies:
         copy.wait_recv()
     left(s_buf, 0)
-    left(z_buf, 1)
-    left(y_buf, 2)
-    left(t_buf, 3)
-    left(others, 4)
-    for copy in scal_copies + rim_copies:
+    left(t_buf, 1)
+    left(others, 2)
+    for copy in swaps + scal_copies + rim_copies:
         copy.wait_send()
+
+
+def refine(block, big, small):
+    fine = jnp.dot(block, big, preferred_element_type=jnp.float32)
+    return fine + jnp.dot(block, small, preferred_element_type=jnp.float32)
 
 
 def weights(field, moved):
@@ -394,15 +396,18 @@
     return total
 
 
-def remesh_kernel(moved, ext, peak, out, swept, landed, shifts):
+def remesh_kernel(moved, wide, ext, peak, block, out, later, swept, landed, shifts):
     top = jnp.max(peak[...], axis=1, keepdims=True)
     top = jnp.max(top, axis=0, keepdims=True)
     scale = COURANT / (top + EPSILON)
 
     def along_x(i, carry):
+        span = pl.ds(pl.multiple_of(8 * STEP * i, 8), 8 * STEP)
+        for c in range(2):
+            later[c, span] = refine(block[span], wide[2 * c], wide[2 * c + 1])
         for tile in range(STEP):
             rows = pl.ds(pl.multiple_of(8 * (STEP * i + tile), 8), 8)
-            total = sweep_roll(ext[rows], scale * moved[0, rows], 1)
+            total = sweep_roll(ext[rows], scale * moved[rows], 1)
             swept[0, rows] = total[:, :128]
             swept[1, rows] = total[:, 128:]
         return carry
@@ -415,7 +420,7 @@
             held = [None] * EY
             for y in range(EY):
                 rows = pl.ds(pl.multiple_of(8 * tile + EZ * y, 8), 8)
-                parts = weights(swept[half, rows], scale * moved[1, rows, lanes])
+                parts = weights(swept[half, rows], scale * later[0, rows, lanes])
                 for target in range(max(y - 6, 0), min(y + 1, FY)):
                     part = parts[target - y + 6]
                     held[target] = part if held[target] is None else held[target] + part
@@ -431,7 +436,7 @@
             lanes = pl.ds(128 * half, 128)
             here = pl.ds(pl.multiple_of(EZ * y, 8), EZ)
             there = pl.ds(pl.multiple_of(EZ * (y + 3), 8), EZ)
-            parts = weights(landed[half, here], scale * moved[2, there, lanes])
+            parts = weights(landed[half, here], scale * later[1, there, lanes])
             total = parts[3][:FZ]
             for k, offset in enumerate((-3, -2, -1, 1, 2, 3)):
                 part = parts[3 + offset]
@@ -455,15 +460,16 @@
     vmem = pl.BlockSpec(memory_space=pltpu.VMEM)
     f32 = jnp.float32
     operands = [vorticity.reshape(3, YB * ZB, N), scalar] + tables
-    moved, ext, peak = pl.pallas_call(
+    moved, wide, ext, peak = pl.pallas_call(
         spectral_kernel,
         out_shape=(
-            pltpu.VMEM((3, EY, EZ, 256), f32),
+            pltpu.VMEM((EY * EZ, 256), f32),
+            pltpu.VMEM((4, 256, 256), jnp.bfloat16),
             pltpu.VMEM((EY, EZ, 256), f32),
             pltpu.VMEM((8, 128), f32),
         ),
         in_specs=[pl.BlockSpec(memory_space=pltpu.HBM)] * len(operands),
-        out_specs=(vmem, vmem, vmem),
+        out_specs=(vmem,) * 4,
         scratch_shapes=[
             pltpu.VMEM((3, 128, 128), f32),
             *[pltpu.VMEM(t.shape, t.dtype) for t in tables],
@@ -479,8 +485,10 @@
             pltpu.VMEM((3, 96, 128), f32),
             pltpu.VMEM((128, 128), f32),
             pltpu.SemaphoreType.DMA((12,)),
-            pltpu.SemaphoreType.DMA((5,)),
-            pltpu.SemaphoreType.DMA((5,)),
+            pltpu.SemaphoreType.DMA((3,)),
+            pltpu.SemaphoreType.DMA((3,)),
+            pltpu.SemaphoreType.DMA((2, 3)),
+            pltpu.SemaphoreType.DMA((2, 3)),
             pltpu.SemaphoreType.DMA((8,)),
             pltpu.SemaphoreType.DMA((8,)),
             pltpu.SemaphoreType.DMA((8,)),
@@ -494,16 +502,17 @@
     return pl.pallas_call(
         remesh_kernel,
         out_shape=jax.ShapeDtypeStruct((FY, FZ, 256), f32),
-        in_specs=[vmem] * 3,
+        in_specs=[vmem] * 5,
         out_specs=vmem,
         scratch_shapes=[
+            pltpu.VMEM((2, EY * EZ, 256), f32),
             pltpu.VMEM((2, EY * EZ, 128), f32),
             pltpu.VMEM((2, FY * EZ, 128), f32),
             pltpu.VMEM((2, 6, 32, 128), f32),
         ],
         compiler_params=pltpu.CompilerParams(vmem_limit_bytes=VMEM_LIMIT),
         name="remesh",
-    )(moved.reshape(3, EY * EZ, 256), ext.reshape(EY * EZ, 256), peak)
+    )(moved, wide, ext.reshape(EY * EZ, 256), peak, tables[-1])
 
 
 def solution(mesh):

time: 39.4 us -> 39.6 us (level)
  no operation moved by 1% of the time
where the time goes in v4:
time: 39.6 us; the launch traced here: 39.4 us
  Pallas kernels  39.4 us (99%)
    pallas_call x1, Pallas kernels, shards(): pl.pallas_call(spectral_kernel, out_shape=(pltpu.VMEM((EY * EZ, 256), f32...  33.1 us
    pallas_call x1, Pallas kernels, shards(): pl.pallas_call(remesh_kernel, out_shape=jax.ShapeDtypeStruct((FY, FZ, 256...  6.32 us

profile of v4, /device:TPU:1, one launch (start us, length us, event | category | flops | bytes accessed | tf_op | source)
XLA Modules:
  0.0 39.4 jit_solution(10030693921806552429)
XLA Ops:
  0.0 0.0 copy-start
  0.0 33.1 %spectral.1 = (f32[912,256]{1,0:T(8,128)S(1)}, bf16[4,256,256]{2,1,0:T(8,128)(2,1)S(1)}, f32[38,24,256]{2,1,0:T(8,128)S(1)}, f32[8,128]{1,0:T(8,128)S(1)}) custom-call(f32[3,128,128]{2,1,0:T(8,128)} %bitcast.3, f32[32,16,256]{2,1,0:T(8,128)} %scal.1, f32[128,128]{1,0:T(8,128)} %constant.20.clone.refs_0_, f32[2,128,128]{2,1,0:T(8,128)} %constant.21.clone.refs_1_, ...), custom_call_target="tpu_custom_call" | custom-call | tf_op jit(solution)/shard_map/spectral/pallas_call | solution.py:463
  33.1 0.0 copy-done
  33.1 6.3 %remesh.1 = f32[32,16,256]{2,1,0:T(8,128)} custom-call(f32[912,256]{1,0:T(8,128)S(1)} %get-tuple-element.9.moved, bf16[4,256,256]{2,1,0:T(8,128)(2,1)S(1)} %get-tuple-element.10.wide, f32[912,256]{1,0:T(8,128)S(1)} %bitcast.2, f32[8,128]{1,0:T(8,128)S(1)} %get-tuple-element.12.peak, bf16[912,256]{1,0:T(8,128)(2,1)S(1)} %copy-done), custom_call_target="tpu_custom_call" | custom-call | tf_op jit(solution)/shard_map/remesh/pallas_call | solution.py:502
Async XLA Ops:
  0.0 33.1 %copy-start = (bf16[912,256]{1,0:T(8,128)(2,1)S(1)}, bf16[912,256]{1,0:T(8,128)(2,1)}, u32[]{:S(2)}) copy-start(bf16[912,256]{1,0:T(8,128)(2,1)} %constant.29.clone.refs_9_.block) | copy-start | bytes 1400836

commit v5 on v4

--- a/solution.py
+++ b/solution.py
@@ -20,7 +20,8 @@
 CHIPS = 64
 YB, ZB = 16, 8
 FY, FZ = 32, 16
-STEP = 19
+LINES = 8
+STEP = 57
 EY, EZ = 38, 24
 
 
@@ -114,7 +115,8 @@
             for y, wy in taps(row - 3):
                 for z, wz in taps(fine_z):
                     block[row * EZ + slot, place[y, z]] += wy * wz
-    return lines.astype(np.float32), block.astype(np.float32)
+    order = np.concatenate([np.arange(0, 2 * N, 2), np.arange(1, 2 * N, 2)])
+    return lines[:, order].astype(np.float32), block.astype(np.float32), np.eye(2 * N)[:, order]
 
 
 def dot(a, b, contract=(1, 0)):
@@ -133,14 +135,19 @@
 )
 
 
+def side_by_side(parts):
+    return jnp.concatenate(parts, axis=1)
+
+
 def spectral_kernel(
     vort_hbm,
     scal,
     *refs,
 ):
-    table_hbm, (moved_out, wide_out, ext_out, peak_out), refs = refs[:10], refs[10:14], refs[14:]
-    vort, tables, refs = refs[0], refs[1:11], refs[11:]
-    fwd_x, fwd_left, twiddle, fwd_right, waves, inv_right, inv_left, inv_x, lines, block = tables
+    table_hbm, (moved_out, wide_out, ext_out, peak_out), refs = refs[:11], refs[11:15], refs[15:]
+    vort, stage, tables, refs = refs[0], refs[1], refs[2:13], refs[13:]
+    fwd_x, fwd_left, twiddle, fwd_right, waves, inv_right, inv_left, inv_x = tables[:8]
+    lines, block, parity = tables[8:]
     s_buf, r_buf, z_buf, zo_buf, y_buf, yo_buf, t_buf, u_buf, rim, pieces, peaks = refs[:11]
     load_sem, send_sem, recv_sem, swap_send, swap_recv = refs[11:16]
     scal_send, scal_recv, rim_send, rim_recv = refs[16:]
@@ -155,14 +162,10 @@
     up_col, down_col = lax.rem(col + 1, COLS), lax.rem(col + COLS - 1, COLS)
 
     loads = [pltpu.make_async_copy(vort_hbm, vort, load_sem.at[0])]
-    for i in range(10):
+    for i in range(11):
         loads.append(pltpu.make_async_copy(table_hbm[i], tables[i], load_sem.at[1 + i]))
-    loads.append(
-        pltpu.make_async_copy(
-            scal, ext_out.at[pl.ds(3, FY), pl.ds(0, FZ), :], load_sem.at[11]
-        )
-    )
-    for load in loads[:2] + loads[11:] + loads[2:11]:
+    loads.append(pltpu.make_async_copy(scal, stage, load_sem.at[12]))
+    for load in loads:
         load.start()
 
     y0, x0 = lax.rem(row, 4), lax.rem(half, 4)
@@ -220,6 +223,14 @@
         pltpu.make_async_copy(source, source, send_sem.at[index]).wait()
 
     exchange(s_buf, r_buf, 0)
+
+    held = stage[...].reshape(FY * FZ, 256)
+    total = jnp.zeros((FY * FZ, 256), jnp.float32)
+    for _ in range(3):
+        piece = held.astype(jnp.bfloat16)
+        held = held - piece.astype(jnp.float32)
+        total = total + jnp.dot(piece, parity[...], preferred_element_type=jnp.float32)
+    ext_out[pl.ds(3, FY), pl.ds(0, FZ), :] = total.reshape(FY, FZ, 256)
 
     def scal_copy(i, ys, zs, yt, zt, device):
         return pltpu.make_async_remote_copy(
@@ -260,40 +271,60 @@
     k_sq = kx * kx + ky * ky + kz * kz
     keep = (k_sq > 0.0) & (ky > -64.0) & (kz > -64.0)
     factor = jnp.where(keep, 1.0 / jnp.maximum(k_sq, 1.0), 0.0) * (1.0 / (N * N * N))
-    omega = []
-    for c in range(3):
-        swaps[c].wait_recv()
+    for copy in swaps:
+        copy.wait_recv()
+    pairs = []
+    for c in range(3):
         joined = z_buf[c] + sign * zo_buf[c]
         re, im = joined[:64], joined[64:]
-        pair = jnp.concatenate([re * tw_re - im * tw_im, re * tw_im + im * tw_re], axis=1)
-        spectrum = dot(pair, fwd_right[...])
-        omega.append((spectrum[:, :128], spectrum[:, 128:]))
+        pairs.append(side_by_side([re * tw_re - im * tw_im, re * tw_im + im * tw_re]))
+    spectrum = dot(jnp.concatenate(pairs), fwd_right[...])
 
     def cross(part):
-        w0, w1, w2 = omega[0][part], omega[1][part], omega[2][part]
+        lanes = slice(128 * part, 128 * part + 128)
+        w0, w1, w2 = spectrum[:64, lanes], spectrum[64:128, lanes], spectrum[128:, lanes]
         return (ky * w2 - kz * w1, kz * w0 - kx * w2, kx * w1 - ky * w0)
 
     cross_re, cross_im = cross(0), cross(1)
-    for c in range(3):
-        pair = jnp.concatenate([-cross_im[c] * factor, cross_re[c] * factor], axis=1)
-        back = dot(pair, inv_right[...])
-        re, im = back[:, :128], back[:, 128:]
+    pairs = [side_by_side([-cross_im[c] * factor, cross_re[c] * factor]) for c in range(3)]
+    back = dot(jnp.concatenate(pairs), inv_right[...])
+    for c in range(3):
+        re, im = back[64 * c : 64 * c + 64, :128], back[64 * c : 64 * c + 64, 128:]
         y_buf[c, :64] = re * tw_re + im * tw_im
         y_buf[c, 64:] = im * tw_re - re * tw_im
         swaps.append(swap(y_buf, yo_buf, 1, c))
-    for c in range(3):
-        swaps[3 + c].wait_recv()
-        joined = y_buf[c] - sign * yo_buf[c]
-        t_buf[c] = dot(inv_left[core], joined).reshape(2, 64, 128)
+    for copy in swaps[3:]:
+        copy.wait_recv()
+    joined = dot(
+        inv_left[core], side_by_side([y_buf[c] - sign * yo_buf[c] for c in range(3)])
+    )
+    for c in range(3):
+        t_buf[c] = joined[:, 128 * c : 128 * c + 128].reshape(2, 64, 128)
     exchange(t_buf, u_buf, 1)
     arrive(u_buf, 1)
     top = jnp.zeros((8, 128), jnp.float32)
-    for c in range(3):
-        velocity = dot(u_buf[c].reshape(128, 128), inv_x[...], (0, 0))
+    joined = dot(
+        side_by_side([u_buf[c].reshape(128, 128) for c in range(3)]), inv_x[...], (0, 0)
+    )
+    for c in range(3):
+        velocity = joined[128 * c : 128 * c + 128]
         rim[c, :128] = velocity
         top = jnp.maximum(top, jnp.max(jnp.abs(velocity).reshape(16, 8, 128), axis=0))
     mine = row * COLS + col
     peaks[pl.ds(mine, 1), :] = jnp.max(top, axis=0, keepdims=True)
+
+    def send_peaks(targets):
+        for device in targets:
+            pltpu.make_async_remote_copy(
+                src_ref=peaks.at[pl.ds(mine, 1), :],
+                dst_ref=peaks.at[pl.ds(mine, 1), :],
+                send_sem=send_sem.at[2],
+                recv_sem=recv_sem.at[2],
+                device_id=device,
+                device_id_type=MESH,
+            ).start()
+
+    send_peaks(devices[:32])
     for c in range(3):
         for i in range(2):
             pieces[c, pl.ds(16 * i, 16), :] = rim[c, pl.ds(6 + i, 16, 8), :]
@@ -325,15 +356,7 @@
     ]
     for copy in rim_copies:
         copy.start()
-    for device in devices:
-        pltpu.make_async_remote_copy(
-            src_ref=peaks.at[pl.ds(mine, 1), :],
-            dst_ref=peaks.at[pl.ds(mine, 1), :],
-            send_sem=send_sem.at[2],
-            recv_sem=recv_sem.at[2],
-            device_id=device,
-            device_id_type=MESH,
-        ).start()
+    send_peaks(devices[32:])
     for copy in rim_copies:
         copy.wait_recv()
     for c in range(3):
@@ -387,13 +410,17 @@
     )
 
 
-def sweep_roll(field, moved, axis):
-    parts = weights(field, moved)
-    length = field.shape[axis]
-    total = parts[3]
-    for offset in (-3, -2, -1, 1, 2, 3):
-        total = total + pltpu.roll(parts[3 + offset], offset % length, axis)
-    return total
+def sweep_x(even, odd, even_moved, odd_moved):
+    e3, e2, e1, e, f1, f2, f3 = weights(even, even_moved)
+    o3, o2, o1, o, p1, p2, p3 = weights(odd, odd_moved)
+
+    def roll(a, shift):
+        return pltpu.roll(a, shift % 128, 1)
+
+    return (
+        (e + o1) + roll(p1 + f2, 1) + roll(e2 + o3, -1) + roll(p3, 2),
+        (o + f1) + roll(e1 + o2, -1) + roll(p2 + f3, 1) + roll(e3, -2),
+    )
 
 
 def remesh_kernel(moved, wide, ext, peak, block, out, later, swept, landed, shifts):
@@ -407,9 +434,12 @@
             later[c, span] = refine(block[span], wide[2 * c], wide[2 * c + 1])
         for tile in range(STEP):
             rows = pl.ds(pl.multiple_of(8 * (STEP * i + tile), 8), 8)
-            total = sweep_roll(ext[rows], scale * moved[rows], 1)
-            swept[0, rows] = total[:, :128]
-            swept[1, rows] = total[:, 128:]
+            swept[0, rows], swept[1, rows] = sweep_x(
+                ext[rows, :128],
+                ext[rows, 128:],
+                scale * moved[rows, :128],
+                scale * moved[rows, 128:],
+            )
         return carry
 
     lax.fori_loop(0, EY * EZ // 8 // STEP, along_x, 0)
@@ -431,32 +461,46 @@
 
         lax.fori_loop(0, EZ // 8, along_y, 0)
 
-    def along_z(y, carry):
-        for half in range(2):
-            lanes = pl.ds(128 * half, 128)
+    lane = lax.broadcasted_iota(jnp.int32, (8, 128), 1)
+    pick = lax.div(lane, 2)
+    is_odd = lax.rem(lane, 2) == 1
+
+    def along_z(i, carry):
+        for step in range(LINES):
+            y = LINES * i + step
             here = pl.ds(pl.multiple_of(EZ * y, 8), EZ)
             there = pl.ds(pl.multiple_of(EZ * (y + 3), 8), EZ)
-            parts = weights(landed[half, here], scale * later[1, there, lanes])
-            total = parts[3][:FZ]
-            for k, offset in enumerate((-3, -2, -1, 1, 2, 3)):
-                part = parts[3 + offset]
-                room = shifts.at[half, k]
-                room[8:24, :] = part[:FZ]
-                if offset > 0:
-                    room[0:8, :] = part[FZ:]
-                else:
-                    room[24:32, :] = part[FZ:]
-                total = total + room[pl.ds(8 - offset, FZ), :]
-            out[y, :, lanes] = total
+            totals = []
+            for half in range(2):
+                lanes = pl.ds(128 * half, 128)
+                parts = weights(landed[half, here], scale * later[1, there, lanes])
+                total = parts[3][:FZ]
+                for k, offset in enumerate((-3, -2, -1, 1, 2, 3)):
+                    part = parts[3 + offset]
+                    room = shifts.at[step, half, k]
+                    room[8:24, :] = part[:FZ]
+                    if offset > 0:
+                        room[0:8, :] = part[FZ:]
+                    else:
+                        room[24:32, :] = part[FZ:]
+                    total = total + room[pl.ds(8 - offset, FZ), :]
+                totals.append(total)
+            for tile in range(FZ // 8):
+                rows = slice(8 * tile, 8 * tile + 8)
+                for half in range(2):
+                    even, odd = (
+                        jnp.take_along_axis(t[rows], pick + 64 * half, axis=1) for t in totals
+                    )
+                    out[y, rows, 128 * half : 128 * half + 128] = jnp.where(is_odd, odd, even)
         return carry
 
-    lax.fori_loop(0, FY, along_z, 0)
+    lax.fori_loop(0, FY // LINES, along_z, 0)
 
 
 def shards(vorticity, scalar):
-    lines, block = refine_tables()
+    lines, block, parity = refine_tables()
     tables = [jnp.asarray(t) for t in spectral_tables() + (lines,)]
-    tables.append(jnp.asarray(block, jnp.bfloat16))
+    tables += [jnp.asarray(block, jnp.bfloat16), jnp.asarray(parity, jnp.bfloat16)]
     vmem = pl.BlockSpec(memory_space=pltpu.VMEM)
     f32 = jnp.float32
     operands = [vorticity.reshape(3, YB * ZB, N), scalar] + tables
@@ -472,6 +516,7 @@
         out_specs=(vmem,) * 4,
         scratch_shapes=[
             pltpu.VMEM((3, 128, 128), f32),
+            pltpu.VMEM((FY, FZ, 256), f32),
             *[pltpu.VMEM(t.shape, t.dtype) for t in tables],
             pltpu.VMEM((3, 2, 64, 128), f32),
             pltpu.VMEM((3, 2, 64, 128), f32),
@@ -484,7 +529,7 @@
             pltpu.VMEM((3, 256, 128), f32),
             pltpu.VMEM((3, 96, 128), f32),
             pltpu.VMEM((128, 128), f32),
-            pltpu.SemaphoreType.DMA((12,)),
+            pltpu.SemaphoreType.DMA((13,)),
             pltpu.SemaphoreType.DMA((3,)),
             pltpu.SemaphoreType.DMA((3,)),
             pltpu.SemaphoreType.DMA((2, 3)),
@@ -508,11 +553,11 @@
             pltpu.VMEM((2, EY * EZ, 256), f32),
             pltpu.VMEM((2, EY * EZ, 128), f32),
             pltpu.VMEM((2, FY * EZ, 128), f32),
-            pltpu.VMEM((2, 6, 32, 128), f32),
+            pltpu.VMEM((LINES, 2, 6, 32, 128), f32),
         ],
         compiler_params=pltpu.CompilerParams(vmem_limit_bytes=VMEM_LIMIT),
         name="remesh",
-    )(moved, wide, ext.reshape(EY * EZ, 256), peak, tables[-1])
+    )(moved, wide, ext.reshape(EY * EZ, 256), peak, tables[-2])
 
 
 def solution(mesh):

time: 39.6 us -> 38.5 us (0.972)
  Pallas kernels: 39.4 us -> 38.4 us
    pallas_call x1, Pallas kernels: 33.1 us -> 32.4 us  [shards(): pl.pallas_call(spectral_kernel, out_shape=(pltpu.VMEM((EY * EZ, 256), f32...]
where the time goes in v5:
time: 38.5 us; the launch traced here: 38.4 us
  Pallas kernels  38.4 us (100%)
    pallas_call x1, Pallas kernels, shards(): pl.pallas_call(spectral_kernel, out_shape=(pltpu.VMEM((EY * EZ, 256), f32...  32.4 us
    pallas_call x1, Pallas kernels, shards(): pl.pallas_call(remesh_kernel, out_shape=jax.ShapeDtypeStruct((FY, FZ, 256...  5.97 us

profile of v5, /device:TPU:1, one launch (start us, length us, event | category | flops | bytes accessed | tf_op | source)
XLA Modules:
  0.0 38.4 jit_solution(12776953225045700900)
XLA Ops:
  0.0 0.0 copy-start
  0.0 32.4 %spectral.1 = (f32[912,256]{1,0:T(8,128)S(1)}, bf16[4,256,256]{2,1,0:T(8,128)(2,1)S(1)}, f32[38,24,256]{2,1,0:T(8,128)S(1)}, f32[8,128]{1,0:T(8,128)S(1)}) custom-call(f32[3,128,128]{2,1,0:T(8,128)} %bitcast.3, f32[32,16,256]{2,1,0:T(8,128)} %scal.1, f32[128,128]{1,0:T(8,128)} %constant.22.clone.refs_0_, f32[2,128,128]{2,1,0:T(8,128)} %constant.23.clone.refs_1_, ...), custom_call_target="tpu_custom_call" | custom-call | tf_op jit(solution)/shard_map/spectral/pallas_call | solution.py:507
  32.4 0.0 copy-done
  32.4 6.0 %remesh.1 = f32[32,16,256]{2,1,0:T(8,128)} custom-call(f32[912,256]{1,0:T(8,128)S(1)} %get-tuple-element.9.moved, bf16[4,256,256]{2,1,0:T(8,128)(2,1)S(1)} %get-tuple-element.10.wide, f32[912,256]{1,0:T(8,128)S(1)} %bitcast.2, f32[8,128]{1,0:T(8,128)S(1)} %get-tuple-element.12.peak, bf16[912,256]{1,0:T(8,128)(2,1)S(1)} %copy-done), custom_call_target="tpu_custom_call" | custom-call | tf_op jit(solution)/shard_map/remesh/pallas_call | solution.py:547
Async XLA Ops:
  0.0 32.4 %copy-start = (bf16[912,256]{1,0:T(8,128)(2,1)S(1)}, bf16[912,256]{1,0:T(8,128)(2,1)}, u32[]{:S(2)}) copy-start(bf16[912,256]{1,0:T(8,128)(2,1)} %constant.31.clone.refs_9_.block) | copy-start | bytes 1400836
